TPU v7x, 128 devices: a whole 4x4x4 slice. The times are simulated.
128 devices in a mesh: gz: 64 (over z, y, x_lo, core), ba: 2 (over x_hi).
Axes of the slice: x: 4 (x_hi: 2, x_lo: 2; x = x_hi * 2 + x_lo), y: 4, z: 4, core: 2. Of those that a mesh axis runs over, the one named last changes fastest.
Arguments:
- coeffs: float32 [2, 3, 4, 128, 128, 128], P(None, None, 'ba', 'gz'), may hold values from -6 to 6
- material: int32 [128, 128, 128], P('gz'), may hold values from 0 to 3
- inv_diag: float32 [4, 3], replicated, may hold values from 0.1 to 1
- inv_off: float32 [4, 3], replicated, may hold values from -0.1 to 0.1
Outputs:
- theta: float32 [2, 3, 4, 128, 128, 128], P(None, None, 'ba', 'gz')
- gram: float32 [2, 4, 4], P(None, None, 'ba')
Inputs may be any that keep to these rules, and one draw needn't show every extreme that they name: material indices.
All inputs are finite; a program needn't handle non-finite values.
Results may differ from a plain program's by a relative error of at most 0.00011.
Values sent between devices are 32-bit elements; how exact they have to be, the bound alone decides.
A program may use at most 64 MiB of HBM per device.

v0:
```python
import jax
import jax.numpy as jnp
import numpy as np
from jax import lax
from jax.experimental import pallas as pl
from jax.experimental.pallas import tpu as pltpu
from jax.sharding import PartitionSpec as P

LOGICAL = pl.DeviceIdType.LOGICAL
N = 128
GZ = 64
DEV = 128
CHUNKS = 3


def reverse_bits_np(values, levels):
    flipped = np.zeros_like(values)
    for position in range(levels):
        flipped = flipped + ((values >> position) & 1) * (1 << (levels - 1 - position))
    return flipped


def as_parts(table):
    high = table.astype(jnp.bfloat16)
    low = (table - high.astype(np.float64)).astype(jnp.bfloat16)
    return np.stack([high, low])


def tables():
    index = np.arange(N)
    scale = 1.0 / np.sqrt(N)
    angle = 2.0 * np.pi / N * (index[:, None] * index[None, :] % N)
    cosine, sine = np.cos(angle) * scale, np.sin(angle) * scale
    first = np.block([[cosine, sine], [-sine, cosine]])
    second = np.block([[cosine, -sine], [sine, cosine]])
    device = np.arange(GZ)
    planes = np.concatenate([device * 2, device * 2 + 1])
    reversed_device = reverse_bits_np(device, 6)
    numbers = np.concatenate([reversed_device, reversed_device + GZ])
    angle = 2.0 * np.pi / N * (planes[:, None] * numbers[None, :] % N)
    cosine, sine = np.cos(angle) * scale, np.sin(angle) * scale
    inverse = np.block([[cosine, -sine], [sine, cosine]])
    return np.stack([as_parts(t) for t in (first, second, inverse, inverse.T)])


def split(values):
    high = values.astype(jnp.bfloat16)
    low = (values - high.astype(jnp.float32)).astype(jnp.bfloat16)
    return high, low


def dot(left, right):
    return jnp.dot(left, right, preferred_element_type=jnp.float32)


def times_table(data, table_ref, which):
    high, low = split(data)
    return dot(high, table_ref[which, 0]) + (dot(low, table_ref[which, 0]) + dot(high, table_ref[which, 1]))


def table_times(table_ref, which, data):
    high, low = split(data)
    return dot(table_ref[which, 0], high) + (dot(table_ref[which, 0], low) + dot(table_ref[which, 1], high))


def swap_blocks(values):
    top = jnp.concatenate([values[:N, :N], values[N:, :N]], axis=1)
    bottom = jnp.concatenate([values[:N, N:], values[N:, N:]], axis=1)
    return jnp.concatenate([top, bottom], axis=0)


def kernel(
    coeffs_hbm, material_hbm, diag_ref, off_ref, tables_hbm,
    theta_hbm, gram_ref,
    coeffs, material, table, work, send1, recv1, field, scaled, send2, recv2, theta,
    material_send, material_recv, gram_send, gram_recv,
    in_sem, out_sem, send_sem, recv_sem,
):
    gz = lax.axis_index("gz")
    ba = lax.axis_index("ba")
    me = gz * 2 + ba
    mine = ba * GZ + gz

    barrier = pltpu.get_barrier_semaphore()

    def greet(i, carry):
        pl.semaphore_signal(barrier, inc=1, device_id=lax.rem(me + 1 + i, DEV), device_id_type=LOGICAL)
        return carry

    loads = [
        pltpu.make_async_copy(coeffs_hbm.at[:, :, band], coeffs.at[band], in_sem.at[band]) for band in range(2)
    ]
    table_load = pltpu.make_async_copy(tables_hbm, table, in_sem.at[2])
    material_load = pltpu.make_async_copy(material_hbm, material, in_sem.at[3])
    loads[0].start()
    table_load.start()
    loads[1].start()
    material_load.start()
    lax.fori_loop(0, DEV - 1, greet, 0, unroll=4)

    qx = lax.broadcasted_iota(jnp.int32, (N, N), 1)
    qx = jnp.where(qx < N // 2, qx, qx - N).astype(jnp.float32) * (1.0 / (N // 2))
    qy = lax.broadcasted_iota(jnp.int32, (N, N), 0)
    qy = jnp.where(qy < N // 2, qy, qy - N).astype(jnp.float32) * (1.0 / (N // 2))
    flipped = 0
    rest = gz
    for _ in range(6):
        flipped = flipped * 2 + lax.rem(rest, 2)
        rest = lax.div(rest, 2)
    qz = [flipped.astype(jnp.float32) * (1.0 / (N // 2)), (flipped - N // 2).astype(jnp.float32) * (1.0 / (N // 2))]

    def curl_of(get, put, sign):
        for plane in range(2):
            for part in range(2):
                hx, hy, hz = get(0, plane, part), get(1, plane, part), get(2, plane, part)
                if sign > 0:
                    put(0, plane, part, qy * hz - qz[plane] * hy)
                    put(1, plane, part, qz[plane] * hx - qx * hz)
                    put(2, plane, part, qx * hy - qy * hx)
                else:
                    put(0, plane, part, qz[plane] * hy - qy * hz)
                    put(1, plane, part, qx * hz - qz[plane] * hx)
                    put(2, plane, part, qy * hx - qx * hy)

    def block(plane, part):
        return pl.ds(plane * N, N), pl.ds(part * N, N)

    def spread(chunk, source, target, base):
        def one(i, carry):
            to = lax.rem(me + 1 + i, DEV)
            row = lax.rem(to, 2) * GZ + lax.div(to, 2)
            pltpu.make_async_remote_copy(
                src_ref=source.at[chunk, pl.ds(pl.multiple_of(row * 8, 8), 8)],
                dst_ref=target.at[chunk, pl.ds(pl.multiple_of(mine * 8, 8), 8)],
                send_sem=send_sem.at[base + chunk],
                recv_sem=recv_sem.at[base + chunk],
                device_id=to,
                device_id_type=LOGICAL,
            ).start()
            return carry

        lax.fori_loop(0, DEV - 1, one, 0, unroll=4)
        own = pl.ds(pl.multiple_of(mine * 8, 8), 8)
        target[chunk, own, :] = source[chunk, own, :]

    def chunk_of_others(ref, sem):
        rows = (DEV - 1) * 8
        return pltpu.make_async_copy(ref.at[0, pl.ds(0, rows)], ref.at[0, pl.ds(0, rows)], sem)

    def forward_xy(q):
        plane_rows = times_table(work[q], table, 0)
        out = table_times(table, 1, swap_blocks(plane_rows))
        for part in range(2):
            for plane in range(2):
                row = (q % 2) * 4 + part * 2 + plane
                send1[q // 2, pl.ds(row, N, stride=8), :] = out[part * N : (part + 1) * N, plane * N : (plane + 1) * N]

    def curl_in(band):
        def get(c, plane, part):
            return coeffs[band, part, c, plane]

        def put(c, plane, part, value):
            rows, lanes = block(plane, part)
            work[band * 3 + c, rows, lanes] = value

        curl_of(get, put, 1)

    loads[0].wait()
    curl_in(0)
    table_load.wait()
    forward_xy(0)
    forward_xy(1)
    pl.semaphore_wait(barrier, DEV - 1)
    spread(0, send1, recv1, 0)

    material_load.wait()
    for plane in range(2):
        material_send[:, plane, :] = material[plane]

    def material_to(i, carry):
        to = lax.rem(gz + 1 + i, GZ)
        pltpu.make_async_remote_copy(
            src_ref=material_send.at[ba * GZ + to],
            dst_ref=material_recv.at[gz],
            send_sem=send_sem.at[6],
            recv_sem=recv_sem.at[6],
            device_id=to * 2 + ba,
            device_id_type=LOGICAL,
        ).start()
        return carry

    lax.fori_loop(0, GZ - 1, material_to, 0, unroll=4)
    material_recv[gz] = material_send[mine]

    loads[1].wait()
    curl_in(1)
    forward_xy(2)
    forward_xy(3)
    spread(1, send1, recv1, 0)
    forward_xy(4)
    forward_xy(5)
    spread(2, send1, recv1, 0)

    def inverse_z(q):
        lines = []
        for part in range(2):
            for plane in range(2):
                row = (q % 2) * 4 + part * 2 + plane
                lines.append(
                    jnp.concatenate(
                        [recv1[q // 2, pl.ds(group * GZ * 8 + row, GZ, stride=8), :] for group in range(2)], axis=1
                    )
                )
        field[q] = table_times(table, 2, jnp.concatenate(lines, axis=0))

    def forward_z(q):
        out = table_times(table, 3, scaled[q])
        for part in range(2):
            for plane in range(2):
                row = (q % 2) * 4 + part * 2 + plane
                start = (part * 2 + plane) * GZ
                for group in range(2):
                    send2[q // 2, pl.ds(group * GZ * 8 + row, GZ, stride=8), :] = out[
                        start : start + GZ, group * N : (group + 1) * N
                    ]

    def entry(k, index):
        ref, column = (diag_ref, k) if k < 3 else (off_ref, k - 3)
        value = jnp.where(index == 1, ref[1, column], ref[0, column])
        value = jnp.where(index == 2, ref[2, column], value)
        return jnp.where(index == 3, ref[3, column], value)

    def apply_material(band):
        for half in range(2):
            index = material_recv[:, half, :]
            xx, yy, zz, xy, yz, zx = [entry(k, index) for k in range(6)]
            for part in range(2):
                for group in range(2):
                    rows, lanes = pl.ds(part * N + half * GZ, GZ), pl.ds(group * N, N)
                    fx, fy, fz = [field[band * 3 + c, rows, lanes] for c in range(3)]
                    scaled[band * 3, rows, lanes] = xx * fx + xy * fy + zx * fz
                    scaled[band * 3 + 1, rows, lanes] = xy * fx + yy * fy + yz * fz
                    scaled[band * 3 + 2, rows, lanes] = zx * fx + yz * fy + zz * fz

    chunk_of_others(recv1, recv_sem.at[0]).wait()
    inverse_z(0)
    inverse_z(1)
    pltpu.make_async_copy(
        material_recv.at[pl.ds(0, GZ - 1)], material_recv.at[pl.ds(0, GZ - 1)], recv_sem.at[6]
    ).wait()
    chunk_of_others(recv1, recv_sem.at[1]).wait()
    inverse_z(2)
    apply_material(0)
    forward_z(0)
    forward_z(1)
    spread(0, send2, recv2, 3)
    forward_z(2)
    inverse_z(3)
    chunk_of_others(recv1, recv_sem.at[2]).wait()
    inverse_z(4)
    inverse_z(5)
    apply_material(1)
    forward_z(3)
    spread(1, send2, recv2, 3)
    forward_z(4)
    forward_z(5)
    spread(2, send2, recv2, 3)

    def gram_step(i, sums):
        sums = list(sums)
        for c in range(3):
            values = []
            for ref in (field, scaled):
                values.append(
                    [
                        [
                            ref[(e % 2) * 3 + c, pl.ds(pl.multiple_of(part * N + i * 8, 8), 8), pl.ds((e // 2) * N, N)]
                            for part in range(2)
                        ]
                        for e in range(4)
                    ]
                )
            f, s = values
            for a in range(4):
                for e in range(4):
                    k = a * 4 + e
                    sums[k] = sums[k] + (f[a][0] * s[e][0] + f[a][1] * s[e][1])
                    sums[16 + k] = sums[16 + k] + (f[a][0] * s[e][1] - f[a][1] * s[e][0])
        return tuple(sums)

    sums = lax.fori_loop(0, N // 8, gram_step, tuple(jnp.zeros((8, N), jnp.float32) for _ in range(32)))
    lane = lax.broadcasted_iota(jnp.int32, (1, N), 1)
    packed = jnp.zeros((1, N), jnp.float32)
    for k in range(32):
        total = jnp.sum(jnp.sum(sums[k], axis=0, keepdims=True), axis=1, keepdims=True)
        packed = packed + jnp.where(lane == k, total, 0.0)
    gram_send[0] = packed
    gram_recv[mine] = packed

    def gram_to(i, carry):
        pltpu.make_async_remote_copy(
            src_ref=gram_send.at[0],
            dst_ref=gram_recv.at[mine],
            send_sem=send_sem.at[7],
            recv_sem=recv_sem.at[7],
            device_id=lax.rem(me + 1 + i, DEV),
            device_id_type=LOGICAL,
        ).start()
        return carry

    lax.fori_loop(0, DEV - 1, gram_to, 0, unroll=4)

    def forward_yx(q):
        halves = []
        for part in range(2):
            halves.append(
                jnp.concatenate(
                    [
                        recv2[q // 2, pl.ds((q % 2) * 4 + part * 2 + plane, N, stride=8), :]
                        for plane in range(2)
                    ],
                    axis=1,
                )
            )
        columns = table_times(table, 0, jnp.concatenate(halves, axis=0))
        work[q] = times_table(swap_blocks(columns), table, 1)

    def curl_out(band):
        def get(c, plane, part):
            rows, lanes = block(plane, part)
            return work[band * 3 + c, rows, lanes]

        def put(c, plane, part, value):
            theta[band, part, c, plane] = value

        curl_of(get, put, -1)

    stores = [
        pltpu.make_async_copy(theta.at[band], theta_hbm.at[:, :, band], out_sem.at[band]) for band in range(2)
    ]
    chunk_of_others(recv2, recv_sem.at[3]).wait()
    forward_yx(0)
    forward_yx(1)
    chunk_of_others(recv2, recv_sem.at[4]).wait()
    forward_yx(2)
    curl_out(0)
    stores[0].start()
    forward_yx(3)
    chunk_of_others(recv2, recv_sem.at[5]).wait()
    forward_yx(4)
    forward_yx(5)
    curl_out(1)
    stores[1].start()

    pltpu.make_async_copy(gram_recv.at[pl.ds(0, DEV - 1)], gram_recv.at[pl.ds(0, DEV - 1)], recv_sem.at[7]).wait()
    whole = jnp.sum(gram_recv[...], axis=0) * (1.0 / (N * N * N))
    across = lax.broadcasted_iota(jnp.int32, (8, N), 1)
    row = lax.broadcasted_iota(jnp.int32, (8, N), 0)
    columns = [
        jnp.sum(jnp.where(across == row * 4 + (ba * 2 + e), whole, 0.0), axis=1, keepdims=True) for e in range(2)
    ]
    gram = jnp.concatenate(columns, axis=1)
    gram_ref[0] = gram[:4]
    gram_ref[1] = gram[4:]

    for chunk in range(CHUNKS):
        chunk_of_others(send1, send_sem.at[chunk]).wait()
        chunk_of_others(send2, send_sem.at[3 + chunk]).wait()
    pltpu.make_async_copy(
        material_send.at[pl.ds(0, GZ - 1)], material_send.at[pl.ds(0, GZ - 1)], send_sem.at[6]
    ).wait()
    pltpu.make_async_copy(gram_recv.at[pl.ds(0, DEV - 1)], gram_recv.at[pl.ds(0, DEV - 1)], send_sem.at[7]).wait()
    stores[0].wait()
    stores[1].wait()


def on_device(coeffs, material, inv_diag, inv_off):
    f32 = jnp.float32
    anywhere = pl.BlockSpec(memory_space=pl.ANY)
    smem = pl.BlockSpec(memory_space=pltpu.SMEM)
    theta, gram = pl.pallas_call(
        kernel,
        out_shape=(jax.ShapeDtypeStruct(coeffs.shape, f32), jax.ShapeDtypeStruct((2, 4, 2), f32)),
        in_specs=[anywhere, anywhere, smem, smem, anywhere],
        out_specs=(anywhere, pl.BlockSpec(memory_space=pltpu.VMEM)),
        scratch_shapes=[
            pltpu.VMEM((2, 2, 3, 2, N, N), f32),
            pltpu.VMEM((2, N, N), jnp.int32),
            pltpu.VMEM((4, 2, 2 * N, 2 * N), jnp.bfloat16),
            pltpu.VMEM((6, 2 * N, 2 * N), f32),
            pltpu.VMEM((CHUNKS, DEV * 8, N), f32),
            pltpu.VMEM((CHUNKS, DEV * 8, N), f32),
            pltpu.VMEM((6, 2 * N, 2 * N), f32),
            pltpu.VMEM((6, 2 * N, 2 * N), f32),
            pltpu.VMEM((CHUNKS, DEV * 8, N), f32),
            pltpu.VMEM((CHUNKS, DEV * 8, N), f32),
            pltpu.VMEM((2, 2, 3, 2, N, N), f32),
            pltpu.VMEM((DEV, 2, N), jnp.int32),
            pltpu.VMEM((GZ, 2, N), jnp.int32),
            pltpu.VMEM((1, 1, N), f32),
            pltpu.VMEM((DEV, 1, N), f32),
            pltpu.SemaphoreType.DMA((4,)),
            pltpu.SemaphoreType.DMA((2,)),
            pltpu.SemaphoreType.DMA((8,)),
            pltpu.SemaphoreType.DMA((8,)),
        ],
        compiler_params=pltpu.CompilerParams(collective_id=0, has_side_effects=True),
        name="maxwell",
    )(coeffs, material, inv_diag, inv_off, jnp.asarray(tables()))
    return theta, gram


def solution(mesh):
    in_specs = (P(None, None, "ba", "gz", None, None), P("gz", None, None), P(), P())
    out_specs = (P(None, None, "ba", "gz", None, None), P(None, None, "ba"))
    return jax.shard_map(
        on_device, mesh=mesh, in_specs=in_specs, out_specs=out_specs, check_vma=False
    )
```

profile of v0, /device:TPU:1, one launch (start us, length us, event | category | flops | bytes accessed | tf_op | source)
XLA Modules:
  0.0 60.1 jit_solution(3399170006217731004)
XLA Ops:
  0.6 55.4 %maxwell.1 = (f32[2,3,2,2,128,128]{5,4,3,2,1,0:T(8,128)}, f32[2,4,2]{2,1,0:T(4,128)}) custom-call(f32[2,3,2,2,128,128]{5,4,3,2,1,0:T(8,128)} %coeffs_hbm.1, s32[2,128,128]{2,1,0:T(8,128)} %material_hbm.1, f32[4,3]{1,0:T(4,128)} %diag_ref.1, f32[4,3]{1,0:T(4,128)} %off_ref.1, bf16[4,2,256,256]{3,2,1,0:T(8,128)(2,1)} %constant.2.clone.tables_hbm), custom_call_target="tpu_custom_call" | custom-call | tf_op jit(solution)/shard_map/maxwell/pallas_call | solution.py:381
  56.0 1.3 %copy.7 = f32[2,4,2]{1,2,0:T(2,128)} copy(f32[2,4,2]{2,1,0:T(4,128)} %get-tuple-element.3) | data formatting | bytes 128 | tf_op jit(solution)/shard_map/maxwell/pallas_call | solution.py:381
  57.4 2.7 %copy.9 = f32[2,3,2,2,128,128]{5,4,3,2,1,0:T(8,128)} copy(f32[2,3,2,2,128,128]{5,4,3,2,1,0:T(8,128)} %get-tuple-element.6) | data formatting | bytes 3145728
where the time goes:
time: 60.3 us; the launch traced here: 60.1 us
  Pallas kernels  55.4 us (92%)
  local copies, waits for them, and re-layouts  4.05 us (7%)
  between operations  0.64 us (1%)
    pallas_call x1, Pallas kernels, on_device(): pl.pallas_call(kernel, out_shape=(jax.ShapeDtypeStruct(coeffs.shape, f32)...  55.4 us
    unnamed x1, local copies, waits for them, and re-layouts  2.7 us
    pallas_call x1, local copies, waits for them, and re-layouts, on_device(): pl.pallas_call(kernel, out_shape=(jax.ShapeDtypeStruct(coeffs.shape, f32)...  1.35 us

commit v1 on v0

v1 whole, which is shorter than its diff:
```python
import jax
import jax.numpy as jnp
import numpy as np
from jax import lax
from jax.experimental import pallas as pl
from jax.experimental.pallas import tpu as pltpu
from jax.sharding import PartitionSpec as P

LOGICAL = pl.DeviceIdType.LOGICAL
N = 128
GZ = 64
DEV = 128
CHUNKS = 3


def reverse_bits_np(values, levels):
    flipped = np.zeros_like(values)
    for position in range(levels):
        flipped = flipped + ((values >> position) & 1) * (1 << (levels - 1 - position))
    return flipped


def as_parts(table):
    high = table.astype(jnp.bfloat16)
    low = (table - high.astype(np.float64)).astype(jnp.bfloat16)
    return np.stack([high, low])


def tables():
    index = np.arange(N)
    scale = 1.0 / np.sqrt(N)
    angle = 2.0 * np.pi / N * (index[:, None] * index[None, :] % N)
    cosine, sine = np.cos(angle) * scale, np.sin(angle) * scale
    first = np.block([[cosine, sine], [-sine, cosine]])
    second = np.block([[cosine, -sine], [sine, cosine]])
    device = np.arange(GZ)
    planes = np.concatenate([device * 2, device * 2 + 1])
    reversed_device = reverse_bits_np(device, 6)
    numbers = np.concatenate([reversed_device, reversed_device + GZ])
    angle = 2.0 * np.pi / N * (planes[:, None] * numbers[None, :] % N)
    cosine, sine = np.cos(angle) * scale, np.sin(angle) * scale
    inverse = np.block([[cosine, -sine], [sine, cosine]])
    return np.stack([as_parts(t) for t in (first, second, inverse, inverse.T)])


def split(values):
    high = values.astype(jnp.bfloat16)
    low = (values - high.astype(jnp.float32)).astype(jnp.bfloat16)
    return high, low


def dot(left, right):
    return jnp.dot(left, right, preferred_element_type=jnp.float32)


def times_table(data, table_ref, which):
    high, low = split(data)
    return dot(high, table_ref[which, 0]) + (dot(low, table_ref[which, 0]) + dot(high, table_ref[which, 1]))


def table_times(table_ref, which, data):
    high, low = split(data)
    return dot(table_ref[which, 0], high) + (dot(table_ref[which, 0], low) + dot(table_ref[which, 1], high))


def swap_blocks(values):
    top = jnp.concatenate([values[:N, :N], values[N:, :N]], axis=1)
    bottom = jnp.concatenate([values[:N, N:], values[N:, N:]], axis=1)
    return jnp.concatenate([top, bottom], axis=0)


def wavevectors(gz):
    qx = lax.broadcasted_iota(jnp.int32, (N, N), 1)
    qx = jnp.where(qx < N // 2, qx, qx - N).astype(jnp.float32) * (1.0 / (N // 2))
    qy = lax.broadcasted_iota(jnp.int32, (N, N), 0)
    qy = jnp.where(qy < N // 2, qy, qy - N).astype(jnp.float32) * (1.0 / (N // 2))
    flipped = 0
    rest = gz
    for _ in range(6):
        flipped = flipped * 2 + lax.rem(rest, 2)
        rest = lax.div(rest, 2)
    qz = [flipped.astype(jnp.float32) * (1.0 / (N // 2)), (flipped - N // 2).astype(jnp.float32) * (1.0 / (N // 2))]
    return qx, qy, qz


def block(plane, part):
    return pl.ds(plane * N, N), pl.ds(part * N, N)


def kernel(
    coeffs_hbm, material_hbm, diag_ref, off_ref, tables_hbm,
    work, sums_ref,
    coeffs, material, table, send1, recv1, field, scaled, send2, recv2,
    material_send, material_recv, tensor, gram_send, gram_recv,
    in_sem, send_sem, recv_sem, group_sem,
):
    gz = lax.axis_index("gz")
    ba = lax.axis_index("ba")
    me = gz * 2 + ba
    mine = ba * GZ + gz

    line, place = lax.div(me, 8), lax.rem(me, 8)
    barrier = pltpu.get_barrier_semaphore()
    places = [lax.rem(place + i, 8) for i in range(8)]
    rows_of = [lax.rem(p, 2) * GZ + lax.div(p, 2) for p in places]

    def line_at(i):
        return lax.rem(line + i, 16)

    for i in range(1, 16):
        pl.semaphore_signal(barrier, inc=1, device_id=line_at(i) * 8 + place, device_id_type=LOGICAL)
    for i in range(1, 8):
        pl.semaphore_signal(barrier, inc=1, device_id=line * 8 + places[i], device_id_type=LOGICAL)

    loads = [
        pltpu.make_async_copy(coeffs_hbm.at[:, :, band], coeffs.at[band], in_sem.at[band]) for band in range(2)
    ]
    table_load = pltpu.make_async_copy(tables_hbm, table, in_sem.at[2])
    material_load = pltpu.make_async_copy(material_hbm, material, in_sem.at[3])
    loads[0].start()
    table_load.start()
    loads[1].start()
    material_load.start()

    qx, qy, qz = wavevectors(gz)

    def to_known(send):
        def one(i, carry):
            there = line_at(i)
            send(there * 8 + place, there * 4 + rows_of[0])
            return carry

        lax.fori_loop(1, 16, one, 0, unroll=5)
        for i in range(1, 8):
            send(line * 8 + places[i], line * 4 + rows_of[i])

    def to_rest(send):
        def one(i, carry):
            there = line_at(i)
            for k in range(1, 8):
                send(there * 8 + places[k], there * 4 + rows_of[k])
            return carry

        lax.fori_loop(1, 16, one, 0)

    def piece(chunk, source, target, base):
        def send(to, row):
            pltpu.make_async_remote_copy(
                src_ref=source.at[chunk, pl.ds(pl.multiple_of(row * 8, 8), 8)],
                dst_ref=target.at[chunk, pl.ds(pl.multiple_of(mine * 8, 8), 8)],
                send_sem=send_sem.at[base + chunk],
                recv_sem=recv_sem.at[base + chunk],
                device_id=to,
                device_id_type=LOGICAL,
            ).start()

        return send

    def keep(chunk, source, target):
        own = pl.ds(pl.multiple_of(mine * 8, 8), 8)
        target[chunk, own, :] = source[chunk, own, :]

    def spread(chunk, source, target, base):
        send = piece(chunk, source, target, base)
        to_known(send)
        to_rest(send)
        keep(chunk, source, target)

    def chunk_of_others(ref, sem):
        rows = (DEV - 1) * 8
        return pltpu.make_async_copy(ref.at[0, pl.ds(0, rows)], ref.at[0, pl.ds(0, rows)], sem)

    def forward_xy(*qs):
        rows = times_table(jnp.concatenate([work[q] for q in qs], axis=0), table, 0)
        blocks = [swap_blocks(rows[i * 2 * N : (i + 1) * 2 * N]) for i in range(len(qs))]
        out = table_times(table, 1, jnp.concatenate(blocks, axis=1))
        for i, q in enumerate(qs):
            for part in range(2):
                for plane in range(2):
                    row = (q % 2) * 4 + part * 2 + plane
                    start = i * 2 * N + plane * N
                    send1[q // 2, pl.ds(row, N, stride=8), :] = out[part * N : (part + 1) * N, start : start + N]

    def curl_in(band):
        for plane in range(2):
            for part in range(2):
                hx, hy, hz = [coeffs[band, part, c, plane] for c in range(3)]
                rows, lanes = block(plane, part)
                work[band * 3, rows, lanes] = qy * hz - qz[plane] * hy
                work[band * 3 + 1, rows, lanes] = qz[plane] * hx - qx * hz
                work[band * 3 + 2, rows, lanes] = qx * hy - qy * hx

    loads[0].wait()
    curl_in(0)
    table_load.wait()
    forward_xy(0, 1)
    pl.semaphore_wait(barrier, 22)
    for i in range(1, 8):
        pl.semaphore_signal(group_sem, inc=1, device_id=line * 8 + places[i], device_id_type=LOGICAL)
    to_known(piece(0, send1, recv1, 0))
    loads[1].wait()
    curl_in(1)
    material_load.wait()
    for plane in range(2):
        material_send[:, plane, :] = material[plane]
    forward_xy(2, 3)
    pl.semaphore_wait(group_sem, 7)
    to_rest(piece(0, send1, recv1, 0))
    keep(0, send1, recv1)

    def material_to(i, carry):
        to = lax.rem(gz + i, GZ)
        pltpu.make_async_remote_copy(
            src_ref=material_send.at[ba * GZ + to],
            dst_ref=material_recv.at[gz],
            send_sem=send_sem.at[6],
            recv_sem=recv_sem.at[6],
            device_id=to * 2 + ba,
            device_id_type=LOGICAL,
        ).start()
        return carry

    lax.fori_loop(1, GZ, material_to, 0, unroll=7)
    material_recv[gz] = material_send[mine]
    spread(1, send1, recv1, 0)
    forward_xy(4, 5)

    def inverse_z(*qs):
        columns = []
        for q in qs:
            lines = []
            for part in range(2):
                for plane in range(2):
                    row = (q % 2) * 4 + part * 2 + plane
                    lines.append(
                        jnp.concatenate(
                            [recv1[q // 2, pl.ds(group * GZ * 8 + row, GZ, stride=8), :] for group in range(2)],
                            axis=1,
                        )
                    )
            columns.append(jnp.concatenate(lines, axis=0))
        out = table_times(table, 2, jnp.concatenate(columns, axis=1))
        for i, q in enumerate(qs):
            field[q] = out[:, i * 2 * N : (i + 1) * 2 * N]

    def forward_z(*qs):
        out = table_times(table, 3, jnp.concatenate([scaled[q] for q in qs], axis=1))
        for i, q in enumerate(qs):
            for part in range(2):
                for plane in range(2):
                    row = (q % 2) * 4 + part * 2 + plane
                    start = (part * 2 + plane) * GZ
                    for group in range(2):
                        lanes = i * 2 * N + group * N
                        send2[q // 2, pl.ds(group * GZ * 8 + row, GZ, stride=8), :] = out[
                            start : start + GZ, lanes : lanes + N
                        ]

    def entry(k, index):
        ref, column = (diag_ref, k) if k < 3 else (off_ref, k - 3)
        value = jnp.where(index == 1, ref[1, column], ref[0, column])
        value = jnp.where(index == 2, ref[2, column], value)
        return jnp.where(index == 3, ref[3, column], value)

    def build_tensor():
        for half in range(2):
            index = material_recv[:, half, :]
            for k in range(6):
                tensor[k, pl.ds(half * GZ, GZ), :] = entry(k, index)

    def apply_material(band):
        for at in range(0, N, 32):
            xx, yy, zz, xy, yz, zx = [tensor[k, pl.ds(at, 32), :] for k in range(6)]
            for part in range(2):
                for group in range(2):
                    rows, lanes = pl.ds(part * N + at, 32), pl.ds(group * N, N)
                    fx, fy, fz = [field[band * 3 + c, rows, lanes] for c in range(3)]
                    scaled[band * 3, rows, lanes] = xx * fx + xy * fy + zx * fz
                    scaled[band * 3 + 1, rows, lanes] = xy * fx + yy * fy + yz * fz
                    scaled[band * 3 + 2, rows, lanes] = zx * fx + yz * fy + zz * fz

    chunk_of_others(recv1, recv_sem.at[0]).wait()
    inverse_z(0, 1)
    spread(2, send1, recv1, 0)
    pltpu.make_async_copy(
        material_recv.at[pl.ds(0, GZ - 1)], material_recv.at[pl.ds(0, GZ - 1)], recv_sem.at[6]
    ).wait()
    build_tensor()
    chunk_of_others(recv1, recv_sem.at[1]).wait()
    inverse_z(2, 3)
    apply_material(0)
    forward_z(0, 1)
    spread(0, send2, recv2, 3)
    chunk_of_others(recv1, recv_sem.at[2]).wait()
    inverse_z(4, 5)
    apply_material(1)
    forward_z(2, 3)
    spread(1, send2, recv2, 3)
    forward_z(4, 5)
    spread(2, send2, recv2, 3)

    def gram_step(i, sums):
        sums = list(sums)
        for c in range(3):
            values = []
            for ref in (field, scaled):
                values.append(
                    [
                        [
                            ref[(e % 2) * 3 + c, pl.ds(pl.multiple_of(part * N + i * 8, 8), 8), pl.ds((e // 2) * N, N)]
                            for part in range(2)
                        ]
                        for e in range(4)
                    ]
                )
            f, s = values
            for a in range(4):
                for e in range(4):
                    k = a * 4 + e
                    sums[k] = sums[k] + (f[a][0] * s[e][0] + f[a][1] * s[e][1])
                    sums[16 + k] = sums[16 + k] + (f[a][0] * s[e][1] - f[a][1] * s[e][0])
        return tuple(sums)

    sums = lax.fori_loop(0, N // 8, gram_step, tuple(jnp.zeros((8, N), jnp.float32) for _ in range(32)))
    lane = lax.broadcasted_iota(jnp.int32, (1, N), 1)
    packed = jnp.zeros((1, N), jnp.float32)
    for k in range(32):
        total = jnp.sum(jnp.sum(sums[k], axis=0, keepdims=True), axis=1, keepdims=True)
        packed = packed + jnp.where(lane == k, total, 0.0)
    gram_send[0] = packed
    gram_recv[mine] = packed

    def gram_to(to, row):
        pltpu.make_async_remote_copy(
            src_ref=gram_send.at[0],
            dst_ref=gram_recv.at[mine],
            send_sem=send_sem.at[7],
            recv_sem=recv_sem.at[7],
            device_id=to,
            device_id_type=LOGICAL,
        ).start()

    to_known(gram_to)
    to_rest(gram_to)

    def forward_yx(*qs):
        columns = []
        for q in qs:
            halves = []
            for part in range(2):
                halves.append(
                    jnp.concatenate(
                        [
                            recv2[q // 2, pl.ds((q % 2) * 4 + part * 2 + plane, N, stride=8), :]
                            for plane in range(2)
                        ],
                        axis=1,
                    )
                )
            columns.append(jnp.concatenate(halves, axis=0))
        out = table_times(table, 0, jnp.concatenate(columns, axis=1))
        blocks = [swap_blocks(out[:, i * 2 * N : (i + 1) * 2 * N]) for i in range(len(qs))]
        rows = times_table(jnp.concatenate(blocks, axis=0), table, 1)
        for i, q in enumerate(qs):
            work[q] = rows[i * 2 * N : (i + 1) * 2 * N]

    chunk_of_others(recv2, recv_sem.at[3]).wait()
    forward_yx(0, 1)
    chunk_of_others(recv2, recv_sem.at[4]).wait()
    forward_yx(2, 3)
    chunk_of_others(recv2, recv_sem.at[5]).wait()
    forward_yx(4, 5)

    pltpu.make_async_copy(gram_recv.at[pl.ds(0, DEV - 1)], gram_recv.at[pl.ds(0, DEV - 1)], recv_sem.at[7]).wait()
    sums_ref[...] = jnp.sum(gram_recv[...], axis=0) * (1.0 / (N * N * N))

    for chunk in range(CHUNKS):
        chunk_of_others(send1, send_sem.at[chunk]).wait()
        chunk_of_others(send2, send_sem.at[3 + chunk]).wait()
    pltpu.make_async_copy(
        material_send.at[pl.ds(0, GZ - 1)], material_send.at[pl.ds(0, GZ - 1)], send_sem.at[6]
    ).wait()
    pltpu.make_async_copy(gram_recv.at[pl.ds(0, DEV - 1)], gram_recv.at[pl.ds(0, DEV - 1)], send_sem.at[7]).wait()


def curl_kernel(work, sums_ref, theta_hbm, gram_ref, theta, out_sem):
    qx, qy, qz = wavevectors(lax.axis_index("gz"))
    stores = []
    for band in range(2):
        for plane in range(2):
            for part in range(2):
                rows, lanes = block(plane, part)
                bx, by, bz = [work[band * 3 + c, rows, lanes] for c in range(3)]
                theta[band, part, 0, plane] = qz[plane] * by - qy * bz
                theta[band, part, 1, plane] = qx * bz - qz[plane] * bx
                theta[band, part, 2, plane] = qy * bx - qx * by
        stores.append(pltpu.make_async_copy(theta.at[band], theta_hbm.at[:, :, band], out_sem.at[band]))
        stores[-1].start()
    first = lax.axis_index("ba") * 2
    lane = lax.broadcasted_iota(jnp.int32, (4, N), 1)
    row = lax.broadcasted_iota(jnp.int32, (4, N), 0)
    start = lax.div(row, 2) * 16 + lax.rem(row, 2) + first
    whole = sums_ref[...]
    columns = [jnp.sum(jnp.where(lane == start + a * 4, whole, 0.0), axis=1, keepdims=True) for a in range(4)]
    gram = jnp.concatenate(columns, axis=1)
    gram_ref[0] = gram[:2]
    gram_ref[1] = gram[2:]
    for store in stores:
        store.wait()


def in_hbm(array):
    return pltpu.with_memory_space_constraint(array, pltpu.HBM)


def on_device(coeffs, material, inv_diag, inv_off):
    f32 = jnp.float32
    anywhere = pl.BlockSpec(memory_space=pltpu.HBM)
    smem = pl.BlockSpec(memory_space=pltpu.SMEM)
    vmem = pl.BlockSpec(memory_space=pltpu.VMEM)
    back, sums = pl.pallas_call(
        kernel,
        out_shape=(jax.ShapeDtypeStruct((6, 2 * N, 2 * N), f32), jax.ShapeDtypeStruct((1, N), f32)),
        in_specs=[anywhere, anywhere, smem, smem, anywhere],
        out_specs=(vmem, vmem),
        scratch_shapes=[
            pltpu.VMEM((2, 2, 3, 2, N, N), f32),
            pltpu.VMEM((2, N, N), jnp.int32),
            pltpu.VMEM((4, 2, 2 * N, 2 * N), jnp.bfloat16),
            pltpu.VMEM((CHUNKS, DEV * 8, N), f32),
            pltpu.VMEM((CHUNKS, DEV * 8, N), f32),
            pltpu.VMEM((6, 2 * N, 2 * N), f32),
            pltpu.VMEM((6, 2 * N, 2 * N), f32),
            pltpu.VMEM((CHUNKS, DEV * 8, N), f32),
            pltpu.VMEM((CHUNKS, DEV * 8, N), f32),
            pltpu.VMEM((DEV, 2, N), jnp.int32),
            pltpu.VMEM((GZ, 2, N), jnp.int32),
            pltpu.VMEM((6, N, N), f32),
            pltpu.VMEM((1, 1, N), f32),
            pltpu.VMEM((DEV, 1, N), f32),
            pltpu.SemaphoreType.DMA((4,)),
            pltpu.SemaphoreType.DMA((8,)),
            pltpu.SemaphoreType.DMA((8,)),
            pltpu.SemaphoreType.REGULAR,
        ],
        compiler_params=pltpu.CompilerParams(
            collective_id=0, has_side_effects=True, vmem_limit_bytes=32 * 1024 * 1024
        ),
        name="maxwell",
    )(in_hbm(coeffs), in_hbm(material), in_hbm(inv_diag), in_hbm(inv_off), in_hbm(jnp.asarray(tables())))
    theta, gram = pl.pallas_call(
        curl_kernel,
        out_shape=(jax.ShapeDtypeStruct(coeffs.shape, f32), jax.ShapeDtypeStruct((2, 2, 4), f32)),
        in_specs=[vmem, vmem],
        out_specs=(anywhere, vmem),
        scratch_shapes=[pltpu.VMEM((2, 2, 3, 2, N, N), f32), pltpu.SemaphoreType.DMA((2,))],
        compiler_params=pltpu.CompilerParams(vmem_limit_bytes=16 * 1024 * 1024),
        name="curl",
    )(back, sums)
    return theta, jnp.transpose(gram, (0, 2, 1))


def solution(mesh):
    in_specs = (P(None, None, "ba", "gz", None, None), P("gz", None, None), P(), P())
    out_specs = (P(None, None, "ba", "gz", None, None), P(None, None, "ba"))
    return jax.shard_map(
        on_device, mesh=mesh, in_specs=in_specs, out_specs=out_specs, check_vma=False
    )
```

time: 60.3 us -> 54.4 us (0.902)
  local copies, waits for them, and re-layouts: 4.05 us -> 0 us
  Pallas kernels: 55.4 us -> 53.6 us
    unnamed x1 -> x0, local copies, waits for them, and re-layouts: 2.7 us -> none
    pallas_call x1 -> x2, Pallas kernels: 55.4 us -> 53.6 us  [the longest x1 51.7 us: on_device(): pl.pallas_call(kernel, out_shape=(jax.ShapeDtypeStruct((6, 2 * N, 2 * N),...]
    pallas_call x1 -> x0, local copies, waits for them, and re-layouts: 1.35 us -> none  [on_device(): pl.pallas_call(kernel, out_shape=(jax.ShapeDtypeStruct(coeffs.shape, f32)...]
where the time goes in v1:
time: 54.4 us; the launch traced here: 54.2 us
  Pallas kernels  53.6 us (99%)
  between operations  0.64 us (1%)
    pallas_call x1, Pallas kernels, on_device(): pl.pallas_call(kernel, out_shape=(jax.ShapeDtypeStruct((6, 2 * N, 2 * N),...  51.7 us
    pallas_call x1, Pallas kernels, on_device(): pl.pallas_call(curl_kernel, out_shape=(jax.ShapeDtypeStruct(coeffs.shape,...  1.86 us

profile of v1, /device:TPU:1, one launch (start us, length us, event | category | flops | bytes accessed | tf_op | source)
XLA Modules:
  0.0 54.2 jit_solution(4824132924091388611)
XLA Ops:
  0.6 51.7 %maxwell.1 = (f32[6,256,256]{2,1,0:T(8,128)S(1)}, f32[1,128]{1,0:T(1,128)S(1)}) custom-call(f32[2,3,2,2,128,128]{5,4,3,2,1,0:T(8,128)} %coeffs_hbm.1, s32[2,128,128]{2,1,0:T(8,128)} %material_hbm.1, f32[4,3]{1,0:T(4,128)} %diag_ref.1, f32[4,3]{1,0:T(4,128)} %off_ref.1, bf16[4,2,256,256]{3,2,1,0:T(8,128)(2,1)} %constant.2.clone.tables_hbm), custom_call_target="tpu_custom_call" | custom-call | tf_op jit(solution)/shard_map/maxwell/pallas_call | solution.py:421
  52.3 1.9 %curl.1 = (f32[2,3,2,2,128,128]{5,4,3,2,1,0:T(8,128)}, f32[2,2,4]{2,1,0:T(2,128)}) custom-call(f32[6,256,256]{2,1,0:T(8,128)S(1)} %get-tuple-element.6.work, f32[1,128]{1,0:T(1,128)S(1)} %get-tuple-element.7.sums_ref), custom_call_target="tpu_custom_call" | custom-call | tf_op jit(solution)/shard_map/curl/pallas_call | solution.py:451

commit v2 on v1

--- a/solution.py
+++ b/solution.py
@@ -11,6 +11,8 @@
 GZ = 64
 DEV = 128
 CHUNKS = 3
+PLACES = ((0, 0), (0, 1), (1, 0), (1, 1), (3, 0), (3, 1), (2, 0), (2, 1))
+SEEN_FROM = (0, 1, 4, 5, 2, 3, 6, 7)
 
 
 def reverse_bits_np(values, levels):
@@ -91,7 +93,7 @@
     coeffs_hbm, material_hbm, diag_ref, off_ref, tables_hbm,
     work, sums_ref,
     coeffs, material, table, send1, recv1, field, scaled, send2, recv2,
-    material_send, material_recv, tensor, gram_send, gram_recv,
+    material_send, material_recv, tensor, gram_send, gram_line, gram_lines,
     in_sem, send_sem, recv_sem, group_sem,
 ):
     gz = lax.axis_index("gz")
@@ -100,8 +102,12 @@
     mine = ba * GZ + gz
 
     line, place = lax.div(me, 8), lax.rem(me, 8)
+    core, across = lax.rem(gz, 2), ba * 2 + lax.rem(lax.div(gz, 2), 2)
     barrier = pltpu.get_barrier_semaphore()
-    places = [lax.rem(place + i, 8) for i in range(8)]
+    places = []
+    for shift, other in PLACES:
+        x = lax.rem(across + shift, 4)
+        places.append(lax.rem(x, 2) * 4 + lax.rem(core + other, 2) * 2 + lax.div(x, 2))
     rows_of = [lax.rem(p, 2) * GZ + lax.div(p, 2) for p in places]
 
     def line_at(i):
@@ -124,32 +130,30 @@
 
     qx, qy, qz = wavevectors(gz)
 
-    def to_known(send):
+    def to_place(send, *which):
         def one(i, carry):
             there = line_at(i)
-            send(there * 8 + place, there * 4 + rows_of[0])
-            return carry
-
-        lax.fori_loop(1, 16, one, 0, unroll=5)
-        for i in range(1, 8):
-            send(line * 8 + places[i], line * 4 + rows_of[i])
-
-    def to_rest(send):
-        def one(i, carry):
-            there = line_at(i)
-            for k in range(1, 8):
+            for k in which:
                 send(there * 8 + places[k], there * 4 + rows_of[k])
             return carry
 
-        lax.fori_loop(1, 16, one, 0)
-
-    def piece(chunk, source, target, base):
+        lax.fori_loop(1, 16, one, 0, unroll=5 if len(which) == 1 else 1)
+
+    def to_line(send, *which):
+        for k in which:
+            send(line * 8 + places[k], line * 4 + rows_of[k])
+
+    def to_all(send):
+        to_place(send, *range(8))
+        to_line(send, *range(1, 8))
+
+    def piece(chunk, source, target, base, arrival=None):
         def send(to, row):
             pltpu.make_async_remote_copy(
                 src_ref=source.at[chunk, pl.ds(pl.multiple_of(row * 8, 8), 8)],
                 dst_ref=target.at[chunk, pl.ds(pl.multiple_of(mine * 8, 8), 8)],
                 send_sem=send_sem.at[base + chunk],
-                recv_sem=recv_sem.at[base + chunk],
+                recv_sem=recv_sem.at[base + chunk if arrival is None else arrival],
                 device_id=to,
                 device_id_type=LOGICAL,
             ).start()
@@ -162,12 +166,11 @@
 
     def spread(chunk, source, target, base):
         send = piece(chunk, source, target, base)
-        to_known(send)
-        to_rest(send)
+        to_all(send)
         keep(chunk, source, target)
 
-    def chunk_of_others(ref, sem):
-        rows = (DEV - 1) * 8
+    def chunk_of_others(ref, sem, count=DEV - 1):
+        rows = count * 8
         return pltpu.make_async_copy(ref.at[0, pl.ds(0, rows)], ref.at[0, pl.ds(0, rows)], sem)
 
     def forward_xy(*qs):
@@ -194,34 +197,62 @@
     curl_in(0)
     table_load.wait()
     forward_xy(0, 1)
-    pl.semaphore_wait(barrier, 22)
-    for i in range(1, 8):
-        pl.semaphore_signal(group_sem, inc=1, device_id=line * 8 + places[i], device_id_type=LOGICAL)
-    to_known(piece(0, send1, recv1, 0))
-    loads[1].wait()
-    curl_in(1)
     material_load.wait()
     for plane in range(2):
         material_send[:, plane, :] = material[plane]
-    forward_xy(2, 3)
-    pl.semaphore_wait(group_sem, 7)
-    to_rest(piece(0, send1, recv1, 0))
-    keep(0, send1, recv1)
-
-    def material_to(i, carry):
-        to = lax.rem(gz + i, GZ)
+
+    def material_to(to, row):
         pltpu.make_async_remote_copy(
-            src_ref=material_send.at[ba * GZ + to],
+            src_ref=material_send.at[row],
             dst_ref=material_recv.at[gz],
             send_sem=send_sem.at[6],
             recv_sem=recv_sem.at[6],
-            device_id=to * 2 + ba,
+            device_id=to,
             device_id_type=LOGICAL,
         ).start()
-        return carry
-
-    lax.fori_loop(1, GZ, material_to, 0, unroll=7)
+
+    def material_to_place(there):
+        start = lax.rem(there, 2) * GZ + lax.div(there, 2)
+
+        def one(i, carry):
+            material_to(line_at(i) * 8 + there, line_at(i) * 4 + start)
+            return carry
+
+        lax.fori_loop(1, 16, one, 0, unroll=5)
+
+    def material_to_line(there):
+        to = line * 8 + there
+        material_to(to, lax.rem(to, 2) * GZ + lax.div(to, 2))
+
+    first = piece(0, send1, recv1, 0)
+    pl.semaphore_wait(barrier, 22)
+    for k in range(1, 8):
+        pl.semaphore_signal(
+            group_sem.at[SEEN_FROM[k]], inc=1, device_id=line * 8 + places[k], device_id_type=LOGICAL
+        )
+    material_to_place(place)
+    to_place(first, 0)
+    to_line(first, *range(1, 8))
+    pl.semaphore_wait(group_sem.at[1], 1)
+    to_place(first, 1)
+    for k in range(2, 4):
+        pl.semaphore_wait(group_sem.at[k], 1)
+    to_place(first, 2, 3)
+    for k in range(4, 6):
+        pl.semaphore_wait(group_sem.at[k], 1)
+    to_place(first, 4, 5)
+    aside = lax.rem(place + 4, 8)
+    for there in (places[1], aside, aside + places[1] - place):
+        material_to_line(there)
+        material_to_place(there)
+    for k in range(6, 8):
+        pl.semaphore_wait(group_sem.at[k], 1)
+    to_place(first, 6, 7)
+    keep(0, send1, recv1)
     material_recv[gz] = material_send[mine]
+    loads[1].wait()
+    curl_in(1)
+    forward_xy(2, 3)
     spread(1, send1, recv1, 0)
     forward_xy(4, 5)
 
@@ -294,10 +325,9 @@
     chunk_of_others(recv1, recv_sem.at[2]).wait()
     inverse_z(4, 5)
     apply_material(1)
+
     forward_z(2, 3)
     spread(1, send2, recv2, 3)
-    forward_z(4, 5)
-    spread(2, send2, recv2, 3)
 
     def gram_step(i, sums):
         sums = list(sums)
@@ -328,20 +358,28 @@
         total = jnp.sum(jnp.sum(sums[k], axis=0, keepdims=True), axis=1, keepdims=True)
         packed = packed + jnp.where(lane == k, total, 0.0)
     gram_send[0] = packed
-    gram_recv[mine] = packed
-
-    def gram_to(to, row):
-        pltpu.make_async_remote_copy(
-            src_ref=gram_send.at[0],
-            dst_ref=gram_recv.at[mine],
-            send_sem=send_sem.at[7],
-            recv_sem=recv_sem.at[7],
-            device_id=to,
-            device_id_type=LOGICAL,
-        ).start()
-
-    to_known(gram_to)
-    to_rest(gram_to)
+    gram_line[place] = packed
+
+    def gram_to(slots, slot, sem):
+        def send(to, row):
+            pltpu.make_async_remote_copy(
+                src_ref=gram_send.at[sem],
+                dst_ref=slots.at[slot],
+                send_sem=send_sem.at[7 + sem],
+                recv_sem=recv_sem.at[7 + sem],
+                device_id=to,
+                device_id_type=LOGICAL,
+            ).start()
+
+        return send
+
+    def gram_wait(slots, count, sem):
+        pltpu.make_async_copy(slots.at[pl.ds(0, count)], slots.at[pl.ds(0, count)], sem).wait()
+
+    to_line(gram_to(gram_line, place, 0), *range(1, 8))
+
+    forward_z(4, 5)
+    spread(2, send2, recv2, 3)
 
     def forward_yx(*qs):
         columns = []
@@ -366,13 +404,18 @@
 
     chunk_of_others(recv2, recv_sem.at[3]).wait()
     forward_yx(0, 1)
+    gram_wait(gram_line, 7, recv_sem.at[7])
+    line_sum = jnp.sum(gram_line[...], axis=0)
+    gram_send[1] = line_sum
+    gram_lines[line] = line_sum
+    to_place(gram_to(gram_lines, line, 1), 0)
     chunk_of_others(recv2, recv_sem.at[4]).wait()
     forward_yx(2, 3)
     chunk_of_others(recv2, recv_sem.at[5]).wait()
     forward_yx(4, 5)
 
-    pltpu.make_async_copy(gram_recv.at[pl.ds(0, DEV - 1)], gram_recv.at[pl.ds(0, DEV - 1)], recv_sem.at[7]).wait()
-    sums_ref[...] = jnp.sum(gram_recv[...], axis=0) * (1.0 / (N * N * N))
+    gram_wait(gram_lines, 15, recv_sem.at[8])
+    sums_ref[...] = jnp.sum(gram_lines[...], axis=0) * (1.0 / (N * N * N))
 
     for chunk in range(CHUNKS):
         chunk_of_others(send1, send_sem.at[chunk]).wait()
@@ -380,7 +423,8 @@
     pltpu.make_async_copy(
         material_send.at[pl.ds(0, GZ - 1)], material_send.at[pl.ds(0, GZ - 1)], send_sem.at[6]
     ).wait()
-    pltpu.make_async_copy(gram_recv.at[pl.ds(0, DEV - 1)], gram_recv.at[pl.ds(0, DEV - 1)], send_sem.at[7]).wait()
+    gram_wait(gram_line, 7, send_sem.at[7])
+    gram_wait(gram_lines, 15, send_sem.at[8])
 
 
 def curl_kernel(work, sums_ref, theta_hbm, gram_ref, theta, out_sem):
@@ -436,12 +480,13 @@
             pltpu.VMEM((DEV, 2, N), jnp.int32),
             pltpu.VMEM((GZ, 2, N), jnp.int32),
             pltpu.VMEM((6, N, N), f32),
-            pltpu.VMEM((1, 1, N), f32),
-            pltpu.VMEM((DEV, 1, N), f32),
+            pltpu.VMEM((2, 1, N), f32),
+            pltpu.VMEM((8, 1, N), f32),
+            pltpu.VMEM((16, 1, N), f32),
             pltpu.SemaphoreType.DMA((4,)),
-            pltpu.SemaphoreType.DMA((8,)),
-            pltpu.SemaphoreType.DMA((8,)),
-            pltpu.SemaphoreType.REGULAR,
+            pltpu.SemaphoreType.DMA((9,)),
+            pltpu.SemaphoreType.DMA((10,)),
+            pltpu.SemaphoreType.REGULAR((8,)),
         ],
         compiler_params=pltpu.CompilerParams(
             collective_id=0, has_side_effects=True, vmem_limit_bytes=32 * 1024 * 1024

time: 54.4 us -> 52.3 us (0.961)
  Pallas kernels: 53.6 us -> 51.5 us
    pallas_call x1, Pallas kernels: 51.7 us -> 49.6 us  [on_device(): pl.pallas_call(kernel, out_shape=(jax.ShapeDtypeStruct((6, 2 * N, 2 * N),...]
where the time goes in v2:
time: 52.3 us; the launch traced here: 52.1 us
  Pallas kernels  51.5 us (98%)
  between operations  0.64 us (1%)
    pallas_call x1, Pallas kernels, on_device(): pl.pallas_call(kernel, out_shape=(jax.ShapeDtypeStruct((6, 2 * N, 2 * N),...  49.6 us
    pallas_call x1, Pallas kernels, on_device(): pl.pallas_call(curl_kernel, out_shape=(jax.ShapeDtypeStruct(coeffs.shape,...  1.86 us

profile of v2, /device:TPU:1, one launch (start us, length us, event | category | flops | bytes accessed | tf_op | source)
XLA Modules:
  0.0 52.1 jit_solution(1163225172958790044)
XLA Ops:
  0.6 49.6 %maxwell.1 = (f32[6,256,256]{2,1,0:T(8,128)S(1)}, f32[1,128]{1,0:T(1,128)S(1)}) custom-call(f32[2,3,2,2,128,128]{5,4,3,2,1,0:T(8,128)} %coeffs_hbm.1, s32[2,128,128]{2,1,0:T(8,128)} %material_hbm.1, f32[4,3]{1,0:T(4,128)} %diag_ref.1, f32[4,3]{1,0:T(4,128)} %off_ref.1, bf16[4,2,256,256]{3,2,1,0:T(8,128)(2,1)} %constant.2.clone.tables_hbm), custom_call_target="tpu_custom_call" | custom-call | tf_op jit(solution)/shard_map/maxwell/pallas_call | solution.py:465
  50.3 1.9 %curl.1 = (f32[2,3,2,2,128,128]{5,4,3,2,1,0:T(8,128)}, f32[2,2,4]{2,1,0:T(2,128)}) custom-call(f32[6,256,256]{2,1,0:T(8,128)S(1)} %get-tuple-element.6.work, f32[1,128]{1,0:T(1,128)S(1)} %get-tuple-element.7.sums_ref), custom_call_target="tpu_custom_call" | custom-call | tf_op jit(solution)/shard_map/curl/pallas_call | solution.py:496

commit v3 on v2

--- a/solution.py
+++ b/solution.py
@@ -90,9 +90,9 @@
 
 
 def kernel(
-    coeffs_hbm, material_hbm, diag_ref, off_ref, tables_hbm,
+    coeffs_hbm, material_hbm, diag_hbm, off_hbm, tables_hbm,
     work, sums_ref,
-    coeffs, material, table, send1, recv1, field, scaled, send2, recv2,
+    coeffs, material, diag_ref, off_ref, table, send1, recv1, field, scaled, send2, recv2,
     material_send, material_recv, tensor, gram_send, gram_line, gram_lines,
     in_sem, send_sem, recv_sem, group_sem,
 ):
@@ -104,17 +104,18 @@
     line, place = lax.div(me, 8), lax.rem(me, 8)
     core, across = lax.rem(gz, 2), ba * 2 + lax.rem(lax.div(gz, 2), 2)
     barrier = pltpu.get_barrier_semaphore()
+
+    def line_at(i):
+        return lax.rem(line + i, 16)
+
+    for i in range(1, 16):
+        pl.semaphore_signal(barrier, inc=1, device_id=line_at(i) * 8 + place, device_id_type=LOGICAL)
     places = []
     for shift, other in PLACES:
         x = lax.rem(across + shift, 4)
         places.append(lax.rem(x, 2) * 4 + lax.rem(core + other, 2) * 2 + lax.div(x, 2))
     rows_of = [lax.rem(p, 2) * GZ + lax.div(p, 2) for p in places]
 
-    def line_at(i):
-        return lax.rem(line + i, 16)
-
-    for i in range(1, 16):
-        pl.semaphore_signal(barrier, inc=1, device_id=line_at(i) * 8 + place, device_id_type=LOGICAL)
     for i in range(1, 8):
         pl.semaphore_signal(barrier, inc=1, device_id=line * 8 + places[i], device_id_type=LOGICAL)
 
@@ -127,6 +128,10 @@
     table_load.start()
     loads[1].start()
     material_load.start()
+    diag_load = pltpu.make_async_copy(diag_hbm, diag_ref, in_sem.at[4])
+    off_load = pltpu.make_async_copy(off_hbm, off_ref, in_sem.at[5])
+    diag_load.start()
+    off_load.start()
 
     qx, qy, qz = wavevectors(gz)
 
@@ -316,6 +321,8 @@
     pltpu.make_async_copy(
         material_recv.at[pl.ds(0, GZ - 1)], material_recv.at[pl.ds(0, GZ - 1)], recv_sem.at[6]
     ).wait()
+    diag_load.wait()
+    off_load.wait()
     build_tensor()
     chunk_of_others(recv1, recv_sem.at[1]).wait()
     inverse_z(2, 3)
@@ -431,15 +438,18 @@
     qx, qy, qz = wavevectors(lax.axis_index("gz"))
     stores = []
     for band in range(2):
-        for plane in range(2):
-            for part in range(2):
+        for part in range(2):
+            for plane in range(2):
                 rows, lanes = block(plane, part)
                 bx, by, bz = [work[band * 3 + c, rows, lanes] for c in range(3)]
                 theta[band, part, 0, plane] = qz[plane] * by - qy * bz
                 theta[band, part, 1, plane] = qx * bz - qz[plane] * bx
                 theta[band, part, 2, plane] = qy * bx - qx * by
-        stores.append(pltpu.make_async_copy(theta.at[band], theta_hbm.at[:, :, band], out_sem.at[band]))
-        stores[-1].start()
+            store = pltpu.make_async_copy(
+                theta.at[band, part], theta_hbm.at[part, :, band], out_sem.at[band * 2 + part]
+            )
+            store.start()
+            stores.append(store)
     first = lax.axis_index("ba") * 2
     lane = lax.broadcasted_iota(jnp.int32, (4, N), 1)
     row = lax.broadcasted_iota(jnp.int32, (4, N), 0)
@@ -460,16 +470,17 @@
 def on_device(coeffs, material, inv_diag, inv_off):
     f32 = jnp.float32
     anywhere = pl.BlockSpec(memory_space=pltpu.HBM)
-    smem = pl.BlockSpec(memory_space=pltpu.SMEM)
     vmem = pl.BlockSpec(memory_space=pltpu.VMEM)
     back, sums = pl.pallas_call(
         kernel,
         out_shape=(jax.ShapeDtypeStruct((6, 2 * N, 2 * N), f32), jax.ShapeDtypeStruct((1, N), f32)),
-        in_specs=[anywhere, anywhere, smem, smem, anywhere],
+        in_specs=[anywhere] * 5,
         out_specs=(vmem, vmem),
         scratch_shapes=[
             pltpu.VMEM((2, 2, 3, 2, N, N), f32),
             pltpu.VMEM((2, N, N), jnp.int32),
+            pltpu.SMEM((4, 3), f32),
+            pltpu.SMEM((4, 3), f32),
             pltpu.VMEM((4, 2, 2 * N, 2 * N), jnp.bfloat16),
             pltpu.VMEM((CHUNKS, DEV * 8, N), f32),
             pltpu.VMEM((CHUNKS, DEV * 8, N), f32),
@@ -483,7 +494,7 @@
             pltpu.VMEM((2, 1, N), f32),
             pltpu.VMEM((8, 1, N), f32),
             pltpu.VMEM((16, 1, N), f32),
-            pltpu.SemaphoreType.DMA((4,)),
+            pltpu.SemaphoreType.DMA((6,)),
             pltpu.SemaphoreType.DMA((9,)),
             pltpu.SemaphoreType.DMA((10,)),
             pltpu.SemaphoreType.REGULAR((8,)),
@@ -498,7 +509,7 @@
         out_shape=(jax.ShapeDtypeStruct(coeffs.shape, f32), jax.ShapeDtypeStruct((2, 2, 4), f32)),
         in_specs=[vmem, vmem],
         out_specs=(anywhere, vmem),
-        scratch_shapes=[pltpu.VMEM((2, 2, 3, 2, N, N), f32), pltpu.SemaphoreType.DMA((2,))],
+        scratch_shapes=[pltpu.VMEM((2, 2, 3, 2, N, N), f32), pltpu.SemaphoreType.DMA((4,))],
         compiler_params=pltpu.CompilerParams(vmem_limit_bytes=16 * 1024 * 1024),
         name="curl",
     )(back, sums)

time: 52.3 us -> 51.5 us (0.985)
  Pallas kernels: 51.5 us -> 50.7 us
    pallas_call x1, Pallas kernels: 49.6 us -> 48.9 us  [on_device(): pl.pallas_call(kernel, out_shape=(jax.ShapeDtypeStruct((6, 2 * N, 2 * N),...]
where the time goes in v3:
time: 51.5 us; the launch traced here: 51.3 us
  Pallas kernels  50.7 us (98%)
  between operations  0.64 us (1%)
    pallas_call x1, Pallas kernels, on_device(): pl.pallas_call(kernel, out_shape=(jax.ShapeDtypeStruct((6, 2 * N, 2 * N),...  48.9 us
    pallas_call x1, Pallas kernels, on_device(): pl.pallas_call(curl_kernel, out_shape=(jax.ShapeDtypeStruct(coeffs.shape,...  1.82 us

profile of v3, /device:TPU:1, one launch (start us, length us, event | category | flops | bytes accessed | tf_op | source)
XLA Modules:
  0.0 51.3 jit_solution(828334987003521529)
XLA Ops:
  0.6 48.9 %maxwell.1 = (f32[6,256,256]{2,1,0:T(8,128)S(1)}, f32[1,128]{1,0:T(1,128)S(1)}) custom-call(f32[2,3,2,2,128,128]{5,4,3,2,1,0:T(8,128)} %coeffs_hbm.1, s32[2,128,128]{2,1,0:T(8,128)} %material_hbm.1, f32[4,3]{1,0:T(4,128)} %diag_hbm.1, f32[4,3]{1,0:T(4,128)} %off_hbm.1, bf16[4,2,256,256]{3,2,1,0:T(8,128)(2,1)} %constant.2.clone.tables_hbm), custom_call_target="tpu_custom_call" | custom-call | tf_op jit(solution)/shard_map/maxwell/pallas_call | solution.py:474
  49.5 1.8 %curl.1 = (f32[2,3,2,2,128,128]{5,4,3,2,1,0:T(8,128)}, f32[2,2,4]{2,1,0:T(2,128)}) custom-call(f32[6,256,256]{2,1,0:T(8,128)S(1)} %get-tuple-element.6.work, f32[1,128]{1,0:T(1,128)S(1)} %get-tuple-element.7.sums_ref), custom_call_target="tpu_custom_call" | custom-call | tf_op jit(solution)/shard_map/curl/pallas_call | solution.py:507

commit v4 on v3

--- a/solution.py
+++ b/solution.py
@@ -108,8 +108,10 @@
     def line_at(i):
         return lax.rem(line + i, 16)
 
-    for i in range(1, 16):
-        pl.semaphore_signal(barrier, inc=1, device_id=line_at(i) * 8 + place, device_id_type=LOGICAL)
+    z, y = lax.div(line, 4), lax.rem(line, 4)
+    for dz, dy in ((2, 2), (2, 1), (2, 3), (1, 2), (3, 2), (2, 0), (0, 2), (1, 1), (1, 3), (3, 1), (3, 3), (1, 0), (3, 0), (0, 1), (0, 3)):
+        there = lax.rem(z + dz, 4) * 4 + lax.rem(y + dy, 4)
+        pl.semaphore_signal(barrier, inc=1, device_id=there * 8 + place, device_id_type=LOGICAL)
     places = []
     for shift, other in PLACES:
         x = lax.rem(across + shift, 4)
@@ -230,8 +232,9 @@
         material_to(to, lax.rem(to, 2) * GZ + lax.div(to, 2))
 
     first = piece(0, send1, recv1, 0)
+    last = piece(0, send1, recv1, 0, 9)
     pl.semaphore_wait(barrier, 22)
-    for k in range(1, 8):
+    for k in (2, 3, 4, 5, 6, 7, 1):
         pl.semaphore_signal(
             group_sem.at[SEEN_FROM[k]], inc=1, device_id=line * 8 + places[k], device_id_type=LOGICAL
         )
@@ -252,7 +255,7 @@
         material_to_place(there)
     for k in range(6, 8):
         pl.semaphore_wait(group_sem.at[k], 1)
-    to_place(first, 6, 7)
+    to_place(last, 6, 7)
     keep(0, send1, recv1)
     material_recv[gz] = material_send[mine]
     loads[1].wait()
@@ -315,9 +318,14 @@
                     scaled[band * 3 + 1, rows, lanes] = xy * fx + yy * fy + yz * fz
                     scaled[band * 3 + 2, rows, lanes] = zx * fx + yz * fy + zz * fz
 
-    chunk_of_others(recv1, recv_sem.at[0]).wait()
+    chunk_of_others(recv1, recv_sem.at[0], 97).wait()
+    third = piece(2, send1, recv1, 0)
+    to_place(third, 4, 5, 6, 7)
+    chunk_of_others(recv1, recv_sem.at[9], 30).wait()
     inverse_z(0, 1)
-    spread(2, send1, recv1, 0)
+    to_place(third, 0, 1, 2, 3)
+    to_line(third, *range(1, 8))
+    keep(2, send1, recv1)
     pltpu.make_async_copy(
         material_recv.at[pl.ds(0, GZ - 1)], material_recv.at[pl.ds(0, GZ - 1)], recv_sem.at[6]
     ).wait()

time: 51.5 us -> 51.5 us (level)
  no operation moved by 1% of the time
where the time goes in v4:
time: 51.5 us; the launch traced here: 51.4 us
  Pallas kernels  50.8 us (99%)
  between operations  0.64 us (1%)
    pallas_call x1, Pallas kernels, on_device(): pl.pallas_call(kernel, out_shape=(jax.ShapeDtypeStruct((6, 2 * N, 2 * N),...  48.9 us
    pallas_call x1, Pallas kernels, on_device(): pl.pallas_call(curl_kernel, out_shape=(jax.ShapeDtypeStruct(coeffs.shape,...  1.82 us

profile of v4, /device:TPU:1, one launch (start us, length us, event | category | flops | bytes accessed | tf_op | source)
XLA Modules:
  0.0 51.4 jit_solution(5709193255257574560)
XLA Ops:
  0.6 48.9 %maxwell.1 = (f32[6,256,256]{2,1,0:T(8,128)S(1)}, f32[1,128]{1,0:T(1,128)S(1)}) custom-call(f32[2,3,2,2,128,128]{5,4,3,2,1,0:T(8,128)} %coeffs_hbm.1, s32[2,128,128]{2,1,0:T(8,128)} %material_hbm.1, f32[4,3]{1,0:T(4,128)} %diag_hbm.1, f32[4,3]{1,0:T(4,128)} %off_hbm.1, bf16[4,2,256,256]{3,2,1,0:T(8,128)(2,1)} %constant.2.clone.tables_hbm), custom_call_target="tpu_custom_call" | custom-call | tf_op jit(solution)/shard_map/maxwell/pallas_call | solution.py:482
  49.6 1.8 %curl.1 = (f32[2,3,2,2,128,128]{5,4,3,2,1,0:T(8,128)}, f32[2,2,4]{2,1,0:T(2,128)}) custom-call(f32[6,256,256]{2,1,0:T(8,128)S(1)} %get-tuple-element.6.work, f32[1,128]{1,0:T(1,128)S(1)} %get-tuple-element.7.sums_ref), custom_call_target="tpu_custom_call" | custom-call | tf_op jit(solution)/shard_map/curl/pallas_call | solution.py:515

commit v5 on v3

--- a/solution.py
+++ b/solution.py
@@ -419,7 +419,8 @@
     chunk_of_others(recv2, recv_sem.at[4]).wait()
     forward_yx(2, 3)
     chunk_of_others(recv2, recv_sem.at[5]).wait()
-    forward_yx(4, 5)
+    forward_yx(4)
+    forward_yx(5)
 
     gram_wait(gram_lines, 15, recv_sem.at[8])
     sums_ref[...] = jnp.sum(gram_lines[...], axis=0) * (1.0 / (N * N * N))

time: 51.5 us -> 51.4 us (level)
  no operation moved by 1% of the time
where the time goes in v5:
time: 51.4 us; the launch traced here: 51.2 us
  Pallas kernels  50.6 us (98%)
  between operations  0.64 us (1%)
    pallas_call x1, Pallas kernels, on_device(): pl.pallas_call(kernel, out_shape=(jax.ShapeDtypeStruct((6, 2 * N, 2 * N),...  48.8 us
    pallas_call x1, Pallas kernels, on_device(): pl.pallas_call(curl_kernel, out_shape=(jax.ShapeDtypeStruct(coeffs.shape,...  1.82 us

profile of v5, /device:TPU:1, one launch (start us, length us, event | category | flops | bytes accessed | tf_op | source)
XLA Modules:
  0.0 51.2 jit_solution(8649773916522383054)
XLA Ops:
  0.6 48.8 %maxwell.1 = (f32[6,256,256]{2,1,0:T(8,128)S(1)}, f32[1,128]{1,0:T(1,128)S(1)}) custom-call(f32[2,3,2,2,128,128]{5,4,3,2,1,0:T(8,128)} %coeffs_hbm.1, s32[2,128,128]{2,1,0:T(8,128)} %material_hbm.1, f32[4,3]{1,0:T(4,128)} %diag_hbm.1, f32[4,3]{1,0:T(4,128)} %off_hbm.1, bf16[4,2,256,256]{3,2,1,0:T(8,128)(2,1)} %constant.2.clone.tables_hbm), custom_call_target="tpu_custom_call" | custom-call | tf_op jit(solution)/shard_map/maxwell/pallas_call | solution.py:475
  49.4 1.8 %curl.1 = (f32[2,3,2,2,128,128]{5,4,3,2,1,0:T(8,128)}, f32[2,2,4]{2,1,0:T(2,128)}) custom-call(f32[6,256,256]{2,1,0:T(8,128)S(1)} %get-tuple-element.6.work, f32[1,128]{1,0:T(1,128)S(1)} %get-tuple-element.7.sums_ref), custom_call_target="tpu_custom_call" | custom-call | tf_op jit(solution)/shard_map/curl/pallas_call | solution.py:508
